TPU v7x, 32 devices: a whole 2x2x4 slice. The times are simulated.
32 devices in a mesh: dp: 16 (over z, x, core), tensor: 2 (over y).
Axes of the slice: x: 2, y: 2, z: 4, core: 2. Of those that a mesh axis runs over, the one named last changes fastest.
Arguments:
- inputs: bfloat16 [16, 256, 4096], P('dp', 'tensor'), may hold values from -40 to 40
- query_states: bfloat16 [16, 256, 3072], P('dp', None, 'tensor'), may hold values from -4.5 to 4.5
- key_states: bfloat16 [16, 256, 1024], P('dp', None, 'tensor'), may hold values from -4.5 to 4.5
- saved_value_states: bfloat16 [16, 256, 1024], P('dp', None, 'tensor'), may hold values from -4.5 to 4.5
- head_cotangent: bfloat16 [16, 256, 3072], P('dp', None, 'tensor'), may hold values from -40 to 40
- query_weight: bfloat16 [4096, 3072], P('dp', 'tensor'), may hold values from -0.09375 to 0.09375
- key_matrix: bfloat16 [4096, 1024], P('dp', 'tensor'), may hold values from -0.09375 to 0.09375
- value_matrix: bfloat16 [4096, 1024], P('dp', 'tensor'), may hold values from -0.09375 to 0.09375
- query_momentum: float32 [4096, 3072], P('dp', 'tensor'), may hold values from -6 to 6
- key_prior_momentum: float32 [4096, 1024], P('dp', 'tensor'), may hold values from -6 to 6
- value_prior_momentum: float32 [4096, 1024], P('dp', 'tensor'), may hold values from -6 to 6
Outputs:
- input_gradient: bfloat16 [16, 256, 4096], P('dp', 'tensor')
- query_velocity: float32 [4096, 3072], P('dp', 'tensor')
- key_velocity: float32 [4096, 1024], P('dp', 'tensor')
- value_velocity: float32 [4096, 1024], P('dp', 'tensor')
All inputs are finite; a program needn't handle non-finite values.
Results may differ from a plain program's by a relative error of at most 0.019.
Values may be sent and summed in bfloat16 or wider, within the bound.
A program may use at most 128 MiB of HBM per device.

v0:
```python
import math

import jax
import jax.numpy as jnp
from jax import lax
from jax.sharding import PartitionSpec as P

MODEL_FEATURES = 4096
QUERY_HEADS = 24
KEY_VALUE_HEADS = 8
HEAD_SIZE = 128


def heads_backward(query_row_set, key_rows, value_rows, cotangent_rows):
    token_length = query_row_set.shape[0]
    kv_heads = key_rows.shape[1] // HEAD_SIZE
    group_width = query_row_set.shape[1] // HEAD_SIZE // kv_heads
    scaling = 1.0 / math.sqrt(HEAD_SIZE)
    query_quad = query_row_set.reshape(token_length, kv_heads, group_width, HEAD_SIZE)
    cotangent_quad = cotangent_rows.reshape(token_length, kv_heads, group_width, HEAD_SIZE)
    key_triple = key_rows.reshape(token_length, kv_heads, HEAD_SIZE)
    value_triple = value_rows.reshape(token_length, kv_heads, HEAD_SIZE)
    block_rows = min(token_length, 512)
    key_sums = jnp.zeros((token_length, kv_heads, HEAD_SIZE), jnp.float32)
    value_sums = jnp.zeros((token_length, kv_heads, HEAD_SIZE), jnp.float32)
    query_blocks = []
    for row_start in range(0, token_length, block_rows):
        row_end = row_start + block_rows
        query_block = query_quad[row_start:row_end]
        cotangent_block = cotangent_quad[row_start:row_end]
        key_block = key_triple[:row_end]
        value_block = value_triple[:row_end]
        scores = (
            jnp.einsum("ihgd,jhd->hgij", query_block, key_block, preferred_element_type=jnp.float32)
            * scaling
        )
        query_index = row_start + lax.broadcasted_iota(jnp.int32, (block_rows, row_end), 0)
        key_index = lax.broadcasted_iota(jnp.int32, (block_rows, row_end), 1)
        scores = jnp.where(query_index >= key_index, scores, -jnp.inf)
        maximum = jnp.max(scores, axis=-1, keepdims=True)
        exponent = jnp.exp(scores - maximum)
        softmax_rows = exponent / jnp.sum(exponent, axis=-1, keepdims=True)
        softmax_reduced = softmax_rows.astype(jnp.bfloat16)
        grad_softmax = jnp.einsum(
            "ihgd,jhd->hgij", cotangent_block, value_block, preferred_element_type=jnp.float32
        )
        row_delta = jnp.sum(softmax_rows * grad_softmax, axis=-1, keepdims=True)
        score_gradient = (softmax_rows * (grad_softmax - row_delta) * scaling).astype(jnp.bfloat16)
        query_blocks.append(
            jnp.einsum(
                "hgij,jhd->ihgd", score_gradient, key_block, preferred_element_type=jnp.float32
            ).astype(jnp.bfloat16)
        )
        key_sums = key_sums.at[:row_end].add(
            jnp.einsum(
                "xfwo,wxfp->oxp", score_gradient, query_block, preferred_element_type=jnp.float32
            )
        )
        value_sums = value_sums.at[:row_end].add(
            jnp.einsum(
                "xfwo,wxfp->oxp",
                softmax_reduced,
                cotangent_block,
                preferred_element_type=jnp.float32,
            )
        )
    grad_query = jnp.concatenate(query_blocks, axis=0).reshape(token_length, -1)
    key_gradient = key_sums.astype(jnp.bfloat16).reshape(token_length, -1)
    value_gradient = value_sums.astype(jnp.bfloat16).reshape(token_length, -1)
    return (grad_query, key_gradient, value_gradient)


def local(
    inputs,
    query_states,
    key_states,
    saved_value_states,
    head_cotangent,
    query_weight,
    key_matrix,
    value_matrix,
    query_momentum,
    key_prior_momentum,
    value_prior_momentum,
):
    query_cols = query_weight.shape[1]
    pair_cols = key_matrix.shape[1]
    local_weights = jnp.concatenate((query_weight, key_matrix, value_matrix), axis=1)
    all_weights = lax.all_gather(local_weights, "dp", axis=0, tiled=True)
    gathered = lax.all_gather(inputs, "tensor", axis=1, tiled=True)[0]
    grad_query, key_gradient, value_gradient = heads_backward(
        query_states[0], key_states[0], saved_value_states[0], head_cotangent[0]
    )
    local_grads = jnp.concatenate((grad_query, key_gradient, value_gradient), axis=1)
    grad_inputs = lax.psum_scatter(
        lax.dot_general(
            local_grads, all_weights, (((1,), (1,)), ((), ())), preferred_element_type=jnp.float32
        ).astype(jnp.bfloat16),
        "tensor",
        scatter_dimension=0,
        tiled=True,
    )[None]
    summed = lax.psum_scatter(
        lax.dot_general(
            gathered, local_grads, (((0,), (0,)), ((), ())), preferred_element_type=jnp.float32
        ).astype(jnp.bfloat16),
        "dp",
        scatter_dimension=0,
        tiled=True,
    ).astype(jnp.float32)
    local_squares = jnp.sum(summed * summed)
    squared_total = lax.psum(local_squares, ("dp", "tensor"))
    summed, squared_total = (summed, squared_total)
    grad_w_query = summed[:, :query_cols]
    grad_w_key = summed[:, query_cols : query_cols + pair_cols]
    grad_w_value = summed[:, query_cols + pair_cols :]
    root_mean_square = jnp.sqrt(
        squared_total / (MODEL_FEATURES * (QUERY_HEADS + 2 * KEY_VALUE_HEADS) * HEAD_SIZE)
    )
    factor = 1.0 / jnp.maximum(root_mean_square, 1.0)
    query_velocity = 0.9 * query_momentum + factor * grad_w_query
    key_velocity = 0.9 * key_prior_momentum + factor * grad_w_key
    value_velocity = 0.9 * value_prior_momentum + factor * grad_w_value
    return (grad_inputs, query_velocity, key_velocity, value_velocity)


def solution(mesh):
    placed = (
        P("dp", "tensor", None),
        P("dp", None, "tensor"),
        P("dp", None, "tensor"),
        P("dp", None, "tensor"),
        P("dp", None, "tensor"),
        P("dp", "tensor"),
        P("dp", "tensor"),
        P("dp", "tensor"),
        P("dp", "tensor"),
        P("dp", "tensor"),
        P("dp", "tensor"),
    )
    return jax.shard_map(
        local,
        mesh=mesh,
        in_specs=placed,
        out_specs=(
            P("dp", "tensor", None),
            P("dp", "tensor"),
            P("dp", "tensor"),
            P("dp", "tensor"),
        ),
        check_vma=False,
    )
```

profile of v0, /device:TPU:0, one launch (start us, length us, event | category | flops | bytes accessed | tf_op | source)
XLA Modules:
  0.0 436.9 jit_solution(14220154882945221395)
XLA Ops:
  7.2 0.7 all-gather.5.cloned.1.call-update
  8.0 2.5 pad_maximum_fusion.1
  10.5 0.0 reduce-scatter.5.cloned.1.call-start
  10.5 0.3 copy.31
  10.8 0.1 reshape_squeeze.12
  10.9 0.2 copy.52
  11.1 0.5 copy-done.2
  11.6 0.3 copy.34
  11.9 0.1 reshape_squeeze.14
  12.0 2.3 fusion.26
  14.2 2.8 fusion.38
  17.0 6.8 %convolution_convert_fusion.2 = bf16[4,3,256,128]{2,3,1,0:T(8,128)(2,1)S(1)} fusion(bf16[256,4,128,1]{0,2,3,1:T(8,128)(2,1)S(1)} %copy.52, f32[4,256,256,3]{2,1,3,0:T(8,128)} %fusion.26, f32[4,3,256,256]{2,3,1,0:T(8,128)} %get-tuple-element.55, f32[4,3,256]{2,1,0:T(4,128)S(1)} %get-tuple-element.54), kind=kOutput, calls=%fused_computation.23 | convolution fusion | flops 207228160 | bytes 7352320 | tf_op jit(solution)/shard_map/hgij,jhd->ihgd/dot_general | solution.py:50
  23.8 5.9 %fusion.20 = bf16[4,256,128]{1,2,0:T(8,128)(2,1)S(1)} fusion(bf16[256,4,3,128]{0,3,2,1:T(8,128)(2,1)S(1)} %bitcast.85, f32[4,256,256,3]{2,1,3,0:T(8,128)} %fusion.26, f32[4,3,256,256]{2,3,1,0:T(8,128)} %get-tuple-element.55, f32[4,3,256]{2,1,0:T(4,128)S(1)} %get-tuple-element.54), kind=kOutput, calls=%fused_computation.30 | convolution fusion | flops 206966016 | bytes 7352320 | tf_op jit(solution)/shard_map/xfwo,wxfp->oxp/dot_general | solution.py:55
  29.7 2.5 fusion.21
  32.3 13.1 %all-gather.5.cloned.1.call-done = bf16[1,256,4096]{2,1,0:T(8,128)(2,1)} async-done(((bf16[1,128,4096]{2,1,0:T(8,128)(2,1)}), bf16[1,256,4096]{2,1,0:T(8,128)(2,1)}) %all-gather.5.cloned.1.call-update) | async-done | bytes 2097168 | tf_op jit(solution)/shard_map/all_gather | solution.py:90
  45.4 13.4 %fusion.2 = bf16[4096,2560]{0,1:T(8,128)(2,1)} fusion(bf16[1,256,4096]{2,1,0:T(8,128)(2,1)} %all-gather.5.cloned.1.call-done, bf16[256,512]{0,1:T(8,128)(2,1)S(1)} %bitcast.88, bf16[256,512]{0,1:T(8,128)(2,1)S(1)} %bitcast.86, bf16[256,1536]{0,1:T(8,128)(2,1)S(1)} %bitcast.82), kind=kOutput, calls=%fused_computation.3 | convolution fusion | flops 5383127040 | bytes 24379392 | tf_op jit(solution)/shard_map/dot_general | solution.py:104
  58.8 0.2 reduce-scatter.3.cloned.1.call-start
  59.0 97.3 %all-gather.3.cloned.1.call-done = bf16[4096,2560]{1,0:T(8,128)(2,1)} async-done(((bf16[256,2560]{1,0:T(8,128)(2,1)}), bf16[4096,2560]{1,0:T(8,128)(2,1)}) %all-gather.3.cloned.1.call-update) | async-done | bytes 20971536 | tf_op jit(solution)/shard_map/all_gather | solution.py:89
  156.3 14.5 %convolution_convert_fusion.1 = bf16[256,4096]{1,0:T(8,128)(2,1)} fusion(bf16[4096,2560]{1,0:T(8,128)(2,1)} %all-gather.3.cloned.1.call-done, bf16[256,512]{0,1:T(8,128)(2,1)S(1)} %bitcast.89, bf16[256,512]{0,1:T(8,128)(2,1)S(1)} %bitcast.87, bf16[256,1536]{0,1:T(8,128)(2,1)S(1)} %bitcast.83), kind=kOutput, calls=%fused_computation.4 | convolution fusion | flops 5373689856 | bytes 24379392 | tf_op jit(solution)/shard_map/dot_general | solution.py:96
  170.9 0.2 copy.42
  171.1 0.9 copy-done.4
  172.0 1.0 copy.43
  173.0 198.8 %reduce-scatter.5.cloned.1.call-done = bf16[256,2560]{0,1:T(8,128)(2,1)} async-done(((bf16[4096,2560]{0,1:T(8,128)(2,1)}), bf16[256,2560]{0,1:T(8,128)(2,1)}) %reduce-scatter.5.cloned.1.call-update) | async-done | bytes 1310736 | tf_op jit(solution)/shard_map/reduce_scatter | solution.py:103
  371.8 2.6 multiply_reduce_fusion
  374.4 1.6 copy.41
  376.0 40.1 %psum.7 = f32[]{:T(128)} all-reduce(f32[]{:T(128)} %multiply_reduce_fusion), channel_id=1, replica_groups=mesh['dp'=16,'tensor'=2] {'dp','tensor'}, use_global_device_ids=true, to_apply=%region_6.7 | all-reduce | flops 1 | bytes 8 | tf_op jit(solution)/shard_map/psum | solution.py:112
  416.8 1.5 convert_element_type.57
  418.3 2.1 fusion.24
  420.5 2.0 copy.45
  422.5 2.0 copy.46
  424.5 2.8 fusion.8
  427.3 3.0 copy.44
  (19 shorter events, 0.2 us)
Async XLA Ops:
  7.2 3.4 copy-start.1
  7.2 38.2 %all-gather.5.cloned.1.call-start = ((), (), s32[]{:S(2)}) async-start(), calls=%async_computation.4 | async-start | bytes 3145728 | tf_op jit(solution)/shard_map/all_gather | solution.py:90
  7.9 2.9 copy-start.5
  7.9 148.4 %all-gather.3.cloned.1.call-start = ((), (), s32[]{:S(2)}) async-start(), calls=%async_computation.2 | async-start | bytes 22282240 | tf_op jit(solution)/shard_map/all_gather | solution.py:89
  10.4 1.1 copy-start.2
  10.4 1.4 copy-start.6
  10.5 361.3 %reduce-scatter.5.cloned.1.call-start = ((), (), s32[]{:S(2)}) async-start(), calls=%async_computation.5 | async-start | bytes 22282240 | tf_op jit(solution)/shard_map/reduce_scatter | solution.py:103
  58.8 112.1 %copy-start.3 = (f32[256,512]{1,0:T(8,128)S(1)}, f32[256,512]{1,0:T(8,128)}, u32[]{:S(2)}) copy-start(f32[256,512]{1,0:T(8,128)} %param.28) | copy-start | bytes 1572868
  58.8 371.5 %reduce-scatter.3.cloned.1.call-start = ((), (), s32[]{:S(2)}) async-start(), calls=%async_computation.3 | async-start | bytes 3145728 | tf_op jit(solution)/shard_map/reduce_scatter | solution.py:95
  170.9 1.1 copy-start.4
  170.9 203.5 %copy-start = (f32[256,1536]{1,0:T(8,128)S(1)}, f32[256,1536]{1,0:T(8,128)}, u32[]{:S(2)}) copy-start(f32[256,1536]{1,0:T(8,128)} %param.27) | copy-start | bytes 4718596
Sparse Core Ops, SparseCore 0:
  9.5 35.8 all-gather.4
  47.5 108.7 all-gather.2
  160.5 211.2 reduce-scatter.4
  374.4 31.7 reduce-scatter.2
where the time goes:
time: 437 us
  waiting for transfers between devices  310 us (71%)
  matrix products  48.2 us (11%)
  blocking collectives  40.1 us (9%)
  between operations  14.6 us (3%)
  local copies, waits for them, and re-layouts  12.1 us (3%)
  other arithmetic  11.5 us (3%)
    reduce_scatter x1, waiting for transfers between devices, local(): lax.psum_scatter(lax.dot_general(gathered, local_grads, (((0,), (0,)), ((...  199 us
    all_gather x1, waiting for transfers between devices, local(): all_weights = lax.all_gather(local_weights, 'dp', axis=0, tiled=True)  97.3 us
    psum x1, blocking collectives, local(): squared_total = lax.psum(local_squares, ('dp', 'tensor'))  40.1 us
    dot_general x1, matrix products, local(): lax.dot_general(local_grads, all_weights, (((1,), (1,)), ((), ())), prefe...  14.5 us
    dot_general x1, matrix products, local(): lax.dot_general(gathered, local_grads, (((0,), (0,)), ((), ())), preferre...  13.4 us
    all_gather x1, waiting for transfers between devices, local(): gathered = lax.all_gather(inputs, 'tensor', axis=1, tiled=True)[0]  13.1 us
    unnamed x22, local copies, waits for them, and re-layouts  11.8 us
  transfers between devices with their start and end apart: 4, of which 3 were waited for; matrix products, arithmetic and copies ran while one was open for 16% of the time, Pallas kernels for 0%

commit v1 on v0

v1 whole, which is shorter than its diff:
```python
import functools
import math

import jax
import jax.numpy as jnp
from jax import lax
from jax.experimental import pallas as pl
from jax.experimental.pallas import tpu as pltpu
from jax.sharding import PartitionSpec as P

HEAD_SIZE = 128
MESH = pl.DeviceIdType.MESH
F32 = jnp.float32
BF16 = jnp.bfloat16


def dot(a, b, ca, cb):
    return lax.dot_general(a, b, (((ca,), (cb,)), ((), ())), preferred_element_type=F32)


def kernel(
    nd, total_entries,
    x_ref, q_ref, k_ref, v_ref, do_ref, wq_ref, wk_ref, wv_ref,
    dx_ref, dwq_ref, dwk_ref, dwv_ref, fac_ref,
    g_all, x_all, w_cat, acc, p_buf, y_buf, d_buf, dxr, sqy, sq,
    xs_s, xs_r, xy_s, xy_r, ring_s, ring_r, dd_s, dd_r, py_s, py_r, dx_s, dx_r,
    sqy_s, sqy_r, sq_s, sq_r,
):
    kv = g_all.shape[1]
    seq = g_all.shape[2]
    wide = g_all.shape[3]
    grp = q_ref.shape[2] // k_ref.shape[2]
    gq = grp * HEAD_SIZE
    rows = wq_ref.shape[0]
    half = seq // 2
    nch = nd // 2
    d = lax.axis_index("dp")
    t = lax.axis_index("tensor")
    c = d % 2
    chip = d // 2
    xx = chip % 2
    zz = chip // 2
    pos = zz * (1 - xx) + (nch - 1 - zz) * xx
    dirn = 1 - 2 * c
    partner = chip * 2 + 1 - c

    def chip_of(p):
        p = (p + 2 * nch) % nch
        h = p // (nch // 2)
        z = p * (1 - h) + (nch - 1 - p) * h
        return 2 * z + h

    nxt = chip_of(pos + dirn) * 2 + c

    def ring_src(k):
        return chip_of(pos - dirn * (k + 1)) * 2 + c

    def partner_src(k):
        return chip_of(pos + dirn * (k + 1)) * 2 + 1 - c

    def to(dp, tt):
        return {"dp": dp, "tensor": tt}

    def rcopy(src, dst, ss, rs, dev):
        return pltpu.make_async_remote_copy(
            src_ref=src, dst_ref=dst, send_sem=ss, recv_sem=rs, device_id=dev, device_id_type=MESH
        )

    bar = pltpu.get_barrier_semaphore()

    def sig(i, _):
        pl.semaphore_signal(bar, inc=1, device_id=to((d + i) % nd, t), device_id_type=MESH)
        return 0

    lax.fori_loop(1, nd, sig, 0)
    pl.semaphore_signal(bar, inc=1, device_id=to(d, 1 - t), device_id_type=MESH)

    for j in range(kv):
        w_cat[j, :, 0:gq] = wq_ref[:, j * gq:(j + 1) * gq]
        w_cat[j, :, gq:gq + HEAD_SIZE] = wk_ref[:, j * HEAD_SIZE:(j + 1) * HEAD_SIZE]
        w_cat[j, :, gq + HEAD_SIZE:wide] = wv_ref[:, j * HEAD_SIZE:(j + 1) * HEAD_SIZE]
    acc[...] = jnp.zeros_like(acc)

    pl.semaphore_wait(bar, nd)

    def xcopy(e, slot):
        return rcopy(
            x_ref.at[0, :, pl.ds(pl.multiple_of(e * rows, 128), rows)],
            x_all.at[slot, t], xs_s.at[e], xs_r.at[slot], to(e, t),
        )

    def xsend(i, _):
        xcopy((d + i) % nd, d).start()
        return 0

    lax.fori_loop(1, nd, xsend, 0)
    x_all[d, t] = x_ref[0, :, pl.ds(pl.multiple_of(d * rows, 128), rows)]

    def xfwd(s):
        return rcopy(x_all.at[s, t], x_all.at[s, t], xy_s.at[s], xy_r.at[s], to(d, 1 - t))

    def xfwd_wait(s):
        rcopy(x_all.at[s, 1 - t], x_all.at[s, 1 - t], xy_s.at[s], xy_r.at[s], to(d, 1 - t)).wait_recv()

    xfwd(d).start()

    def ring(step, j, s):
        return rcopy(g_all.at[s, j], g_all.at[s, j], ring_s.at[step, j], ring_r.at[step, j], to(nxt, t))

    def d2d(step, j, s):
        return rcopy(g_all.at[s, j], g_all.at[s, j], dd_s.at[step, j], dd_r.at[step, j], to(partner, t))

    scaling = 1.0 / math.sqrt(HEAD_SIZE)

    def attention(j, _):
        kk = k_ref[0, :, pl.ds(pl.multiple_of(j * HEAD_SIZE, 128), HEAD_SIZE)]
        vv = v_ref[0, :, pl.ds(pl.multiple_of(j * HEAD_SIZE, 128), HEAD_SIZE)]
        dk = jnp.zeros((seq, HEAD_SIZE), F32)
        dv = jnp.zeros((seq, HEAD_SIZE), F32)
        mask = lax.broadcasted_iota(jnp.int32, (seq, seq), 0) >= lax.broadcasted_iota(
            jnp.int32, (seq, seq), 1
        )
        for g in range(grp):
            cols = pl.ds(pl.multiple_of(j * gq + g * HEAD_SIZE, 128), HEAD_SIZE)
            qq = q_ref[0, :, cols]
            oo = do_ref[0, :, cols]
            s = jnp.where(mask, dot(qq, kk, 1, 1) * scaling, -jnp.inf)
            e = jnp.exp(s - jnp.max(s, axis=-1, keepdims=True))
            soft = e / jnp.sum(e, axis=-1, keepdims=True)
            gs = dot(oo, vv, 1, 1)
            delta = jnp.sum(soft * gs, axis=-1, keepdims=True)
            ds = (soft * (gs - delta) * scaling).astype(BF16)
            g_all[d, j, :, g * HEAD_SIZE:(g + 1) * HEAD_SIZE] = dot(ds, kk, 1, 0).astype(BF16)
            dk = dk + dot(ds, qq, 0, 0)
            dv = dv + dot(soft.astype(BF16), oo, 0, 0)
        g_all[d, j, :, gq:gq + HEAD_SIZE] = dk.astype(BF16)
        g_all[d, j, :, gq + HEAD_SIZE:wide] = dv.astype(BF16)
        ring(0, j, d).start()
        d2d(0, j, d).start()
        return 0

    lax.fori_loop(0, kv, attention, 0)

    def xready(s):
        xcopy(s, s).wait_recv()
        xfwd(s).start()

    def pcopy(s):
        return rcopy(p_buf.at[s, 1 - t], y_buf.at[s], py_s.at[s], py_r.at[s], to(d, 1 - t))

    def block(s):
        xfwd_wait(s)
        xb = x_all[s].reshape(seq, rows)
        part = jnp.zeros((seq, rows), F32)
        for j in range(kv):
            gb = g_all[s, j]
            part = part + dot(gb, w_cat[j], 1, 1)
            acc[j] += dot(xb, gb, 0, 0)
        p_buf[s] = part.astype(BF16).reshape(2, half, rows)
        pcopy(s).start()

    def reduced(s):
        pcopy(s).wait_recv()
        return (p_buf[s, t].astype(F32) + y_buf[s].astype(F32)).astype(BF16)

    def dxcopy(s, slot):
        return rcopy(d_buf.at[s], dxr.at[slot], dx_s.at[s], dx_r.at[slot], to(s, t))

    def finish(s):
        d_buf[s] = reduced(s)
        dxcopy(s, d).start()

    xready(partner)
    block(d)
    for j in range(kv):
        d2d(0, j, partner).wait_recv()
    block(partner)
    dxr[d] = reduced(d)
    steps = nch - 1

    def step(k, _):
        sa = ring_src(k)
        sb = partner_src(k)
        xready(sa)
        xready(sb)
        for j in range(kv):
            ring(k, j, sa).wait_recv()

            @pl.when(k < steps - 1)
            def _():
                ring(k + 1, j, sa).start()

            d2d(k + 1, j, sa).start()
        block(sa)
        for j in range(kv):
            d2d(k + 1, j, sb).wait_recv()
        block(sb)

        @pl.when(k == 0)
        def _():
            finish(partner)

        @pl.when(k > 0)
        def _():
            finish(ring_src(k - 1))
            finish(partner_src(k - 1))

        return 0

    lax.fori_loop(0, steps, step, 0)

    squares = jnp.zeros((1, 1), F32)
    for j in range(kv):
        a = acc[j]
        squares = squares + jnp.sum(a * a, keepdims=True)
    sqy[t] = jnp.broadcast_to(squares, (8, 128))
    sqc = rcopy(sqy.at[t], sqy.at[t], sqy_s, sqy_r, to(d, 1 - t))
    sqc.start()
    finish(ring_src(steps - 1))
    finish(partner_src(steps - 1))
    rcopy(sqy.at[1 - t], sqy.at[1 - t], sqy_s, sqy_r, to(d, 1 - t)).wait_recv()
    sq[d] = sqy[0] + sqy[1]

    def sqcopy(e, slot):
        return rcopy(sq.at[slot], sq.at[slot], sq_s.at[e], sq_r.at[slot], to(e, t))

    def sqsend(i, _):
        sqcopy((d + i) % nd, d).start()
        return 0

    lax.fori_loop(1, nd, sqsend, 0)
    for j in range(kv):
        dwq_ref[:, j * gq:(j + 1) * gq] = acc[j, :, 0:gq]
        dwk_ref[:, j * HEAD_SIZE:(j + 1) * HEAD_SIZE] = acc[j, :, gq:gq + HEAD_SIZE]
        dwv_ref[:, j * HEAD_SIZE:(j + 1) * HEAD_SIZE] = acc[j, :, gq + HEAD_SIZE:wide]

    def drain(i, _):
        e = (d + i) % nd
        xcopy(e, d).wait_send()
        dxcopy(e, d).wait_send()
        dxcopy(e, e).wait_recv()
        sqcopy(e, d).wait_send()
        sqcopy(e, e).wait_recv()
        return 0

    lax.fori_loop(1, nd, drain, 0)

    def drain_all(s, _):
        xfwd(s).wait_send()
        pcopy(s).wait_send()
        return 0

    lax.fori_loop(0, nd, drain_all, 0)
    sqc.wait_send()
    for j in range(kv):
        def drain_g(k, _):
            ring(k, j, d).wait_send()
            d2d(k, j, d).wait_send()
            return 0

        lax.fori_loop(0, steps, drain_g, 0)
        d2d(steps, j, d).wait_send()
    for e in range(nd):
        dx_ref[0, :, e * rows:(e + 1) * rows] = dxr[e]
    total = jnp.sum(sq[...], axis=0)
    fac_ref[...] = 1.0 / jnp.maximum(jnp.sqrt(total / total_entries), 1.0)


def fused(nd, nt, inputs, q, k, v, do, wq, wk, wv):
    seq = q.shape[1]
    kv = k.shape[2] // HEAD_SIZE
    wide = (q.shape[2] + 2 * k.shape[2]) // kv
    rows = wq.shape[0]
    half = seq // nt
    total_entries = float(rows * nd * kv * wide * nt)
    vm = pl.BlockSpec(memory_space=pltpu.VMEM)
    dma = pltpu.SemaphoreType.DMA
    steps = nd // 2 - 1
    return pl.pallas_call(
        functools.partial(kernel, nd, total_entries),
        out_shape=(
            jax.ShapeDtypeStruct(inputs.shape, BF16),
            jax.ShapeDtypeStruct(wq.shape, F32),
            jax.ShapeDtypeStruct(wk.shape, F32),
            jax.ShapeDtypeStruct(wv.shape, F32),
            jax.ShapeDtypeStruct((8, 128), F32),
        ),
        in_specs=[vm] * 8,
        out_specs=(vm,) * 5,
        scratch_shapes=[
            pltpu.VMEM((nd, kv, seq, wide), BF16),
            pltpu.VMEM((nd, nt, half, rows), BF16),
            pltpu.VMEM((kv, rows, wide), BF16),
            pltpu.VMEM((kv, rows, wide), F32),
            pltpu.VMEM((nd, nt, half, rows), BF16),
            pltpu.VMEM((nd, half, rows), BF16),
            pltpu.VMEM((nd, half, rows), BF16),
            pltpu.VMEM((nd, half, rows), BF16),
            pltpu.VMEM((2, 8, 128), F32),
            pltpu.VMEM((nd, 8, 128), F32),
            dma((nd,)), dma((nd,)), dma((nd,)), dma((nd,)),
            dma((steps, kv)), dma((steps, kv)), dma((steps + 1, kv)), dma((steps + 1, kv)),
            dma((nd,)), dma((nd,)), dma((nd,)), dma((nd,)),
            dma, dma, dma((nd,)), dma((nd,)),
        ],
        compiler_params=pltpu.CompilerParams(
            collective_id=0, has_side_effects=True, vmem_limit_bytes=60 * 1024 * 1024
        ),
    )(inputs, q, k, v, do, wq, wk, wv)


def heads_backward(query_row_set, key_rows, value_rows, cotangent_rows):
    token_length = query_row_set.shape[0]
    kv_heads = key_rows.shape[1] // HEAD_SIZE
    group_width = query_row_set.shape[1] // HEAD_SIZE // kv_heads
    scaling = 1.0 / math.sqrt(HEAD_SIZE)
    query_quad = query_row_set.reshape(token_length, kv_heads, group_width, HEAD_SIZE)
    cotangent_quad = cotangent_rows.reshape(token_length, kv_heads, group_width, HEAD_SIZE)
    key_triple = key_rows.reshape(token_length, kv_heads, HEAD_SIZE)
    value_triple = value_rows.reshape(token_length, kv_heads, HEAD_SIZE)
    block_rows = min(token_length, 512)
    key_sums = jnp.zeros((token_length, kv_heads, HEAD_SIZE), F32)
    value_sums = jnp.zeros((token_length, kv_heads, HEAD_SIZE), F32)
    query_blocks = []
    for row_start in range(0, token_length, block_rows):
        row_end = row_start + block_rows
        query_block = query_quad[row_start:row_end]
        cotangent_block = cotangent_quad[row_start:row_end]
        key_block = key_triple[:row_end]
        value_block = value_triple[:row_end]
        scores = (
            jnp.einsum("ihgd,jhd->hgij", query_block, key_block, preferred_element_type=F32)
            * scaling
        )
        query_index = row_start + lax.broadcasted_iota(jnp.int32, (block_rows, row_end), 0)
        key_index = lax.broadcasted_iota(jnp.int32, (block_rows, row_end), 1)
        scores = jnp.where(query_index >= key_index, scores, -jnp.inf)
        maximum = jnp.max(scores, axis=-1, keepdims=True)
        exponent = jnp.exp(scores - maximum)
        softmax_rows = exponent / jnp.sum(exponent, axis=-1, keepdims=True)
        softmax_reduced = softmax_rows.astype(BF16)
        grad_softmax = jnp.einsum(
            "ihgd,jhd->hgij", cotangent_block, value_block, preferred_element_type=F32
        )
        row_delta = jnp.sum(softmax_rows * grad_softmax, axis=-1, keepdims=True)
        score_gradient = (softmax_rows * (grad_softmax - row_delta) * scaling).astype(BF16)
        query_blocks.append(
            jnp.einsum(
                "hgij,jhd->ihgd", score_gradient, key_block, preferred_element_type=F32
            ).astype(BF16)
        )
        key_sums = key_sums.at[:row_end].add(
            jnp.einsum(
                "xfwo,wxfp->oxp", score_gradient, query_block, preferred_element_type=F32
            )
        )
        value_sums = value_sums.at[:row_end].add(
            jnp.einsum(
                "xfwo,wxfp->oxp",
                softmax_reduced,
                cotangent_block,
                preferred_element_type=F32,
            )
        )
    grad_query = jnp.concatenate(query_blocks, axis=0).reshape(token_length, -1)
    key_gradient = key_sums.astype(BF16).reshape(token_length, -1)
    value_gradient = value_sums.astype(BF16).reshape(token_length, -1)
    return (grad_query, key_gradient, value_gradient)


def small(nd, nt, inputs, query_states, key_states, query_weight):
    seq = query_states.shape[1]
    cols = query_states.shape[2] + 2 * key_states.shape[2]
    held = nd * seq * cols * 2 + 10 * nd * seq * query_weight.shape[0]
    return nt == 2 and nd % 4 == 0 and nd >= 8 and held < 36 * 1024 * 1024


def local(nd, nt, *args):
    inputs, q, k, v, do, wq, wk, wv, mq, mk, mv = args
    if small(nd, nt, inputs, q, k, wq):
        grad_inputs, gq, gk, gv, fac = fused(nd, nt, inputs, q, k, v, do, wq, wk, wv)
        factor = fac[0, 0]
    else:
        query_cols = wq.shape[1]
        pair_cols = wk.shape[1]
        rows = wq.shape[0]
        weights = jnp.concatenate((wq, wk, wv), axis=1)
        grads = jnp.concatenate(heads_backward(q[0], k[0], v[0], do[0]), axis=1)
        all_grads = lax.all_gather(grads, "dp", axis=0, tiled=True)
        pieces = lax.all_to_all(inputs[0], "dp", 1, 0, tiled=True)
        pieces = pieces.reshape(nd, -1, rows)
        all_inputs = lax.all_gather(pieces, "tensor", axis=1, tiled=True).reshape(-1, rows)
        summed = dot(all_inputs, all_grads, 0, 0)
        parts = dot(all_grads, weights, 1, 1).astype(BF16).reshape(nd, -1, rows)
        mine = lax.psum_scatter(parts, "tensor", scatter_dimension=1, tiled=True)
        grad_inputs = lax.all_to_all(mine.reshape(-1, rows), "dp", 0, 1, tiled=True)[None]
        total = lax.psum(jnp.sum(summed * summed), ("dp", "tensor"))
        factor = 1.0 / jnp.maximum(jnp.sqrt(total / (summed.size * nd * nt)), 1.0)
        gq = summed[:, :query_cols]
        gk = summed[:, query_cols:query_cols + pair_cols]
        gv = summed[:, query_cols + pair_cols:]
    return (
        grad_inputs,
        0.9 * mq + factor * gq,
        0.9 * mk + factor * gk,
        0.9 * mv + factor * gv,
    )


def solution(mesh):
    nd, nt = mesh.shape["dp"], mesh.shape["tensor"]
    saved = P("dp", None, "tensor")
    tokens = P("dp", "tensor", None)
    weight = P("dp", "tensor")
    return jax.shard_map(
        functools.partial(local, nd, nt),
        mesh=mesh,
        in_specs=(tokens,) + (saved,) * 4 + (weight,) * 6,
        out_specs=(tokens,) + (weight,) * 3,
        check_vma=False,
    )
```

time: 437 us -> 174 us (0.40)
  waiting for transfers between devices: 310 us -> 0 us
  Pallas kernels: 0 us -> 166 us
  matrix products: 48.2 us -> 0 us
  blocking collectives: 40.1 us -> 0 us
  between operations: 14.6 us -> 0.67 us
  local copies, waits for them, and re-layouts: 12.1 us -> 2.18 us
  other arithmetic: 11.5 us -> 5.5 us
    reduce_scatter x2 -> x0, waiting for transfers between devices: 199 us -> none  [the longest x1 199 us: local(): lax.psum_scatter(lax.dot_general(gathered, local_grads, (((0,), (0,)), ((...]
    pallas_call x0 -> x1, Pallas kernels: none -> 166 us  [fused(): pl.pallas_call(functools.partial(kernel, nd, total_entries), out_shape=(j...]
    all_gather x2 -> x0, waiting for transfers between devices: 110 us -> none  [the longest x1 97.3 us: local(): all_weights = lax.all_gather(local_weights, 'dp', axis=0, tiled=True)]
    dot_general x6 -> x0, matrix products: 45.4 us -> none  [the longest x1 14.5 us: local(): lax.dot_general(local_grads, all_weights, (((1,), (1,)), ((), ())), prefe...]
    psum x1 -> x0, blocking collectives: 40.1 us -> none  [local(): squared_total = lax.psum(local_squares, ('dp', 'tensor'))]
    unnamed x22 -> x11, local copies, waits for them, and re-layouts: 11.8 us -> 0.99 us
  transfers between devices with their start and end apart: 4 -> 0, of which waited for: 3 -> 0; matrix products, arithmetic and copies ran while one was open for 16% -> 0% of each run, Pallas kernels for 0% -> 0%
where the time goes in v1:
time: 174 us
  Pallas kernels  166 us (95%)
  other arithmetic  5.5 us (3%)
  local copies, waits for them, and re-layouts  2.18 us (1%)
    pallas_call x1, Pallas kernels, fused(): pl.pallas_call(functools.partial(kernel, nd, total_entries), out_shape=(j...  166 us

profile of v1, /device:TPU:0, one launch (start us, length us, event | category | flops | bytes accessed | tf_op | source)
XLA Modules:
  0.0 174.2 jit_solution(10928261799036791986)
XLA Ops:
  0.6 0.0 copy-start.3
  0.6 0.0 copy-start.4
  0.7 165.9 %shard_map.138 = (bf16[1,128,4096]{2,1,0:T(8,128)(2,1)}, f32[256,1536]{1,0:T(8,128)}, f32[256,512]{1,0:T(8,128)}, f32[256,512]{1,0:T(8,128)}, f32[8,128]{1,0:T(8,128)}) custom-call(bf16[1,128,4096]{2,1,0:T(8,128)(2,1)} %x_ref.1, bf16[1,256,1536]{2,1,0:T(8,128)(2,1)} %q_ref.1, bf16[1,256,512]{2,1,0:T(8,128)(2,1)} %k_ref.1, bf16[1,256,512]{2,1,0:T(8,128)(2,1)} %v_ref.1, ...), custom_call_target="tpu_custom_call" | custom-call | tf_op jit(solution)/shard_map/pallas_call | solution.py:279
  166.6 1.2 slice.3
  167.7 0.0 copy-done.3
  167.7 0.0 copy-done.4
  167.7 0.0 copy-start
  167.8 0.0 copy-start.1
  167.8 3.4 %multiply_add_fusion.1 = (f32[256,512]{1,0:T(8,128)}, f32[256,512]{1,0:T(8,128)}) fusion(f32[256,512]{1,0:T(8,128)} %get-tuple-element.13, f32[256,512]{1,0:T(8,128)S(1)} %copy-done.3, f32[]{:T(128)} %bitcast, f32[256,512]{1,0:T(8,128)} %get-tuple-element.12, f32[256,512]{1,0:T(8,128)S(1)} %copy-done.4), kind=kLoop, calls=%fused_computation.1 | loop fusion | flops 786432 | bytes 3145732 | tf_op jit(solution)/shard_map/add | solution.py:406
  171.1 0.0 copy-done
  171.1 0.0 copy-done.1
  171.1 0.0 copy-start.2
  171.1 2.1 %multiply_add_fusion = f32[256,1536]{1,0:T(8,128)} fusion(f32[256,1536]{1,0:T(8,128)S(1)} %copy-done.1, f32[256,1536]{1,0:T(8,128)S(1)} %copy-done, f32[]{:T(128)} %bitcast), kind=kLoop, calls=%fused_computation | loop fusion | flops 1179648 | bytes 4718596 | tf_op jit(solution)/shard_map/add | solution.py:404
  173.3 0.0 copy-done.2
  173.3 1.0 copy.16
Async XLA Ops:
  0.6 167.1 %copy-start.3 = (f32[256,512]{1,0:T(8,128)S(1)}, f32[256,512]{1,0:T(8,128)}, u32[]{:S(2)}) copy-start(f32[256,512]{1,0:T(8,128)} %param.21) | copy-start | bytes 1572868
  0.6 167.1 %copy-start.4 = (f32[256,512]{1,0:T(8,128)S(1)}, f32[256,512]{1,0:T(8,128)}, u32[]{:S(2)}) copy-start(f32[256,512]{1,0:T(8,128)} %param.20) | copy-start | bytes 1572868
  167.7 3.4 %copy-start = (f32[256,1536]{1,0:T(8,128)S(1)}, f32[256,1536]{1,0:T(8,128)}, u32[]{:S(2)}) copy-start(f32[256,1536]{1,0:T(8,128)} %param.19) | copy-start | bytes 4718596
  167.8 3.4 %copy-start.1 = (f32[256,1536]{1,0:T(8,128)S(1)}, f32[256,1536]{1,0:T(8,128)}, u32[]{:S(2)}) copy-start(f32[256,1536]{1,0:T(8,128)} %get-tuple-element.11) | copy-start | bytes 4718596
  171.1 2.2 %copy-start.2 = (bf16[1,128,4096]{2,1,0:T(8,128)(2,1)S(1)}, bf16[1,128,4096]{2,1,0:T(8,128)(2,1)}, u32[]{:S(2)}) copy-start(bf16[1,128,4096]{2,1,0:T(8,128)(2,1)} %get-tuple-element.20) | copy-start | bytes 3145732

commit v2 on v1

--- a/solution.py
+++ b/solution.py
@@ -22,7 +22,7 @@
     nd, total_entries,
     x_ref, q_ref, k_ref, v_ref, do_ref, wq_ref, wk_ref, wv_ref,
     dx_ref, dwq_ref, dwk_ref, dwv_ref, fac_ref,
-    g_all, x_all, w_cat, acc, p_buf, y_buf, d_buf, dxr, sqy, sq,
+    g_all, x_all, w_cat, acc, p_buf, y_buf, d_buf, dxr, sqy, sq, xt, part,
     xs_s, xs_r, xy_s, xy_r, ring_s, ring_r, dd_s, dd_r, py_s, py_r, dx_s, dx_r,
     sqy_s, sqy_r, sq_s, sq_r,
 ):
@@ -148,16 +148,24 @@
     def pcopy(s):
         return rcopy(p_buf.at[s, 1 - t], y_buf.at[s], py_s.at[s], py_r.at[s], to(d, 1 - t))
 
-    def block(s):
-        xfwd_wait(s)
-        xb = x_all[s].reshape(seq, rows)
-        part = jnp.zeros((seq, rows), F32)
-        for j in range(kv):
-            gb = g_all[s, j]
-            part = part + dot(gb, w_cat[j], 1, 1)
-            acc[j] += dot(xb, gb, 0, 0)
-        p_buf[s] = part.astype(BF16).reshape(2, half, rows)
-        pcopy(s).start()
+    def load_x(a, b):
+        for n, s in enumerate((a, b)):
+            xfwd_wait(s)
+            xt[n] = x_all[s].reshape(seq, rows).T
+
+    def chunk(j, a, b):
+        ga = g_all[a, j]
+        gb = g_all[b, j]
+        acc[j] += dot(xt[0], ga, 1, 0) + dot(xt[1], gb, 1, 0)
+        pa = dot(ga, w_cat[j], 1, 1)
+        pb = dot(gb, w_cat[j], 1, 1)
+        part[0] = pa if j == 0 else part[0] + pa
+        part[1] = pb if j == 0 else part[1] + pb
+
+    def send_parts(a, b):
+        for n, s in enumerate((a, b)):
+            p_buf[s] = part[n].astype(BF16).reshape(2, half, rows)
+            pcopy(s).start()
 
     def reduced(s):
         pcopy(s).wait_recv()
@@ -170,13 +178,35 @@
         d_buf[s] = reduced(s)
         dxcopy(s, d).start()
 
+    steps = nch - 1
+
+    def arrive(k, j, sa):
+        ring(k, j, sa).wait_recv()
+
+        @pl.when(k < steps - 1)
+        def _():
+            ring(k + 1, j, sa).start()
+
+        d2d(k + 1, j, sa).start()
+
     xready(partner)
-    block(d)
-    for j in range(kv):
+    sa = ring_src(0)
+    sb = partner_src(0)
+    xready(sa)
+    xready(sb)
+    load_x(d, partner)
+    for j in range(kv):
+        arrive(0, j, sa)
         d2d(0, j, partner).wait_recv()
-    block(partner)
+        chunk(j, d, partner)
+    send_parts(d, partner)
+    load_x(sa, sb)
+    for j in range(kv):
+        d2d(1, j, sb).wait_recv()
+        chunk(j, sa, sb)
+    send_parts(sa, sb)
     dxr[d] = reduced(d)
-    steps = nch - 1
+    finish(partner)
 
     def step(k, _):
         sa = ring_src(k)
@@ -184,30 +214,18 @@
         xready(sa)
         xready(sb)
         for j in range(kv):
-            ring(k, j, sa).wait_recv()
-
-            @pl.when(k < steps - 1)
-            def _():
-                ring(k + 1, j, sa).start()
-
-            d2d(k + 1, j, sa).start()
-        block(sa)
-        for j in range(kv):
+            arrive(k, j, sa)
+            if j == 0:
+                load_x(sa, sb)
             d2d(k + 1, j, sb).wait_recv()
-        block(sb)
-
-        @pl.when(k == 0)
-        def _():
-            finish(partner)
-
-        @pl.when(k > 0)
-        def _():
-            finish(ring_src(k - 1))
-            finish(partner_src(k - 1))
-
-        return 0
-
-    lax.fori_loop(0, steps, step, 0)
+            chunk(j, sa, sb)
+            if j == 0:
+                finish(ring_src(k - 1))
+                finish(partner_src(k - 1))
+        send_parts(sa, sb)
+        return 0
+
+    lax.fori_loop(1, steps, step, 0)
 
     squares = jnp.zeros((1, 1), F32)
     for j in range(kv):
@@ -298,6 +316,8 @@
             pltpu.VMEM((nd, half, rows), BF16),
             pltpu.VMEM((2, 8, 128), F32),
             pltpu.VMEM((nd, 8, 128), F32),
+            pltpu.VMEM((2, rows, seq), BF16),
+            pltpu.VMEM((2, seq, rows), F32),
             dma((nd,)), dma((nd,)), dma((nd,)), dma((nd,)),
             dma((steps, kv)), dma((steps, kv)), dma((steps + 1, kv)), dma((steps + 1, kv)),
             dma((nd,)), dma((nd,)), dma((nd,)), dma((nd,)),

time: 174 us -> 175 us (level)
  no operation moved by 1% of the time
where the time goes in v2:
time: 175 us
  Pallas kernels  167 us (95%)
  other arithmetic  5.5 us (3%)
  local copies, waits for them, and re-layouts  2.18 us (1%)
    pallas_call x1, Pallas kernels, fused(): pl.pallas_call(functools.partial(kernel, nd, total_entries), out_shape=(j...  167 us

profile of v2, /device:TPU:0, one launch (start us, length us, event | category | flops | bytes accessed | tf_op | source)
XLA Modules:
  0.0 175.0 jit_solution(17607459232157740516)
XLA Ops:
  0.6 0.0 copy-start.3
  0.6 0.0 copy-start.4
  0.7 166.6 %shard_map.138 = (bf16[1,128,4096]{2,1,0:T(8,128)(2,1)}, f32[256,1536]{1,0:T(8,128)}, f32[256,512]{1,0:T(8,128)}, f32[256,512]{1,0:T(8,128)}, f32[8,128]{1,0:T(8,128)}) custom-call(bf16[1,128,4096]{2,1,0:T(8,128)(2,1)} %x_ref.1, bf16[1,256,1536]{2,1,0:T(8,128)(2,1)} %q_ref.1, bf16[1,256,512]{2,1,0:T(8,128)(2,1)} %k_ref.1, bf16[1,256,512]{2,1,0:T(8,128)(2,1)} %v_ref.1, ...), custom_call_target="tpu_custom_call" | custom-call | tf_op jit(solution)/shard_map/pallas_call | solution.py:297
  167.3 1.2 slice.3
  168.5 0.0 copy-done.3
  168.5 0.0 copy-done.4
  168.5 0.0 copy-start
  168.5 0.0 copy-start.1
  168.5 3.4 %multiply_add_fusion.1 = (f32[256,512]{1,0:T(8,128)}, f32[256,512]{1,0:T(8,128)}) fusion(f32[256,512]{1,0:T(8,128)} %get-tuple-element.13, f32[256,512]{1,0:T(8,128)S(1)} %copy-done.3, f32[]{:T(128)} %bitcast, f32[256,512]{1,0:T(8,128)} %get-tuple-element.12, f32[256,512]{1,0:T(8,128)S(1)} %copy-done.4), kind=kLoop, calls=%fused_computation.1 | loop fusion | flops 786432 | bytes 3145732 | tf_op jit(solution)/shard_map/add | solution.py:426
  171.8 0.0 copy-done
  171.8 0.0 copy-done.1
  171.8 0.0 copy-start.2
  171.8 2.1 %multiply_add_fusion = f32[256,1536]{1,0:T(8,128)} fusion(f32[256,1536]{1,0:T(8,128)S(1)} %copy-done.1, f32[256,1536]{1,0:T(8,128)S(1)} %copy-done, f32[]{:T(128)} %bitcast), kind=kLoop, calls=%fused_computation | loop fusion | flops 1179648 | bytes 4718596 | tf_op jit(solution)/shard_map/add | solution.py:424
  174.0 0.0 copy-done.2
  174.0 1.0 copy.16
Async XLA Ops:
  0.6 167.8 %copy-start.3 = (f32[256,512]{1,0:T(8,128)S(1)}, f32[256,512]{1,0:T(8,128)}, u32[]{:S(2)}) copy-start(f32[256,512]{1,0:T(8,128)} %param.21) | copy-start | bytes 1572868
  0.6 167.8 %copy-start.4 = (f32[256,512]{1,0:T(8,128)S(1)}, f32[256,512]{1,0:T(8,128)}, u32[]{:S(2)}) copy-start(f32[256,512]{1,0:T(8,128)} %param.20) | copy-start | bytes 1572868
  168.5 3.4 %copy-start = (f32[256,1536]{1,0:T(8,128)S(1)}, f32[256,1536]{1,0:T(8,128)}, u32[]{:S(2)}) copy-start(f32[256,1536]{1,0:T(8,128)} %param.19) | copy-start | bytes 4718596
  168.5 3.4 %copy-start.1 = (f32[256,1536]{1,0:T(8,128)S(1)}, f32[256,1536]{1,0:T(8,128)}, u32[]{:S(2)}) copy-start(f32[256,1536]{1,0:T(8,128)} %get-tuple-element.11) | copy-start | bytes 4718596
  171.8 2.2 %copy-start.2 = (bf16[1,128,4096]{2,1,0:T(8,128)(2,1)S(1)}, bf16[1,128,4096]{2,1,0:T(8,128)(2,1)}, u32[]{:S(2)}) copy-start(bf16[1,128,4096]{2,1,0:T(8,128)(2,1)} %get-tuple-element.20) | copy-start | bytes 3145732
